TPU v7x, 32 devices: a whole 2x2x4 slice. The times are simulated.
32 devices in a mesh: grp: 4 (over z), dev: 8 (over y, x, core).
Axes of the slice: x: 2, y: 2, z: 4, core: 2. Of those that a mesh axis runs over, the one named last changes fastest.
Arguments:
- amounts: float32 [64, 524288], P('dev', 'grp'), may hold values from -0.06 to 0.06, as said below
Outputs:
- offsets: float32 [64, 524288], P(None, ('grp', 'dev'))
Inputs may be any that keep to these rules, and one draw needn't show every extreme that they name: `amounts`: each entry lies within 0.06 of zero.
All inputs are finite; a program needn't handle non-finite values.
Results may differ from a plain program's by a relative error of at most 0.00095.
Values sent between devices are 32-bit elements; how exact they have to be, the bound alone decides.
A program may use at most 64 MiB of HBM per device.

v0:
```python
import jax
import jax.numpy as jnp
from jax import lax
from jax.sharding import PartitionSpec as P


def carried_in(value, axis, join, neutral):
    count, mine = (lax.axis_size(axis), lax.axis_index(axis))
    pieces = lax.all_gather(value, axis)
    total = jnp.full_like(value, 0) + jnp.asarray(neutral, value.dtype)

    def lap(position, total):
        longer = join(total, pieces[position])
        return jnp.where(position < mine, longer, total)

    return lax.fori_loop(0, count - 1, lap, total)


def local_scan(values):
    chans, length = values.shape
    block_len = 512
    count = length // block_len
    row_index = lax.broadcasted_iota(jnp.int32, (block_len, block_len), 0)
    col_index = lax.broadcasted_iota(jnp.int32, (block_len, block_len), 1)
    upper_ones = (row_index < col_index).astype(jnp.float32)
    blocks = values.reshape(chans * count, block_len)
    within = jnp.dot(
        blocks, upper_ones, precision=lax.Precision.HIGHEST, preferred_element_type=jnp.float32
    )
    within = within.reshape(chans, count, block_len)
    sums = jnp.sum(values.reshape(chans, count, block_len), axis=2)
    starts = jnp.cumsum(sums, axis=1) - sums
    result = (within + starts[:, :, None]).reshape(chans, length)
    return (result, jnp.sum(sums, axis=1))


def combine(earlier, later):
    return earlier + later


def relayout(values):
    return lax.all_to_all(values, "dev", split_axis=1, concat_axis=0, tiled=True)


def chain_groups(column_sum):
    return carried_in(column_sum, "grp", combine, jnp.zeros_like(column_sum))


def local(amounts):
    partial_sums, column_sum = local_scan(amounts)
    result = relayout(partial_sums + chain_groups(column_sum)[:, None])
    return result


def solution(mesh):
    return jax.shard_map(
        local,
        mesh=mesh,
        in_specs=(P("dev", "grp"),),
        out_specs=P(None, ("grp", "dev")),
        check_vma=False,
    )
```

profile of v0, /device:TPU:0, one launch (start us, length us, event | category | flops | bytes accessed | tf_op | source)
XLA Modules:
  0.0 113.7 jit_solution(17269614239907794902)
XLA Ops:
  0.0 4.9 %reshape.45 = f32[2048,512]{1,0:T(8,128)} reshape(f32[8,131072]{1,0:T(8,128)} %param.3) | data formatting | bytes 8388608 | tf_op jit(solution)/shard_map/reshape | solution.py:26
  4.9 8.2 %convolution_bitcast_fusion = f32[2048,512]{0,1:T(8,128)} fusion(f32[2048,512]{1,0:T(8,128)} %reshape.45), kind=kOutput, calls=%fused_computation.3 | convolution fusion | flops 6442975232 | bytes 8388608 | tf_op jit(solution)/shard_map/dot_general | solution.py:27
  13.1 5.3 %copy.14 = f32[2048,512]{1,0:T(8,128)} copy(f32[2048,512]{0,1:T(8,128)} %convolution_bitcast_fusion) | data formatting | bytes 8388608 | tf_op jit(solution)/shard_map/dot_general | solution.py:27
  18.5 4.9 %reshape.46 = f32[8,8,16384]{2,1,0:T(8,128)} reshape(f32[2048,512]{1,0:T(8,128)} %copy.14) | data formatting | bytes 8388608 | tf_op jit(solution)/shard_map/reshape | solution.py:30
  23.4 3.4 %reduce_sum.19 = f32[8]{0:T(128)S(1)} reduce(f32[8,131072]{1,0:T(8,128)} %param.3, f32[]{:T(128)} %constant.32.clone.1), dimensions={1}, to_apply=%region_3.4 | reduce | flops 1048568 | bytes 4194340 | tf_op jit(solution)/shard_map/reduce_sum | solution.py:34
  26.8 2.5 %reduce_sum.18 = f32[8,256]{0,1:T(8,128)S(1)} reduce(f32[8,256,512]{2,0,1:T(8,128)} %bitcast.15, f32[]{:T(128)} %constant.32.clone.1), dimensions={2}, to_apply=%region_0.0 | reduce | flops 1046528 | bytes 4202500 | tf_op jit(solution)/shard_map/reduce_sum | solution.py:31
  29.3 0.1 copy.16
  29.4 0.1 copy.15
  29.5 0.6 reduce-window.6
  30.0 0.2 slice_reduce_fusion
  30.2 0.1 bitcast_subtract_fusion
  30.3 2.4 %add.49 = f32[8,256,512]{2,1,0:T(8,128)} broadcast(f32[8,256]{1,0:T(8,128)S(1)} %bitcast_subtract_fusion), dimensions={0,1} | broadcast | bytes 4202496 | tf_op jit(solution)/shard_map/add | solution.py:33
  32.7 0.0 copy-start
  32.7 5.0 %add.50 = f32[8,8,16384]{2,1,0:T(8,128)} reshape(f32[8,256,512]{2,1,0:T(8,128)} %add.49) | data formatting | bytes 8388608 | tf_op jit(solution)/shard_map/add | solution.py:33
  37.7 0.0 copy-done
  37.7 0.6 dynamic-slice
  38.9 0.2 dynamic-update-slice
  39.1 13.5 %all-reduce = f32[32]{0:T(128)S(1)} all-reduce(f32[32]{0:T(128)S(1)} %dynamic-update-slice), channel_id=2, replica_groups=mesh['grp'=4,'dev'=8] {'grp'}, use_global_device_ids=true, to_apply=%add | all-reduce | flops 32 | bytes 256
  52.6 0.1 reshape.50
  52.7 0.1 while.14
  52.8 3.9 %add_add_fusion = f32[8,8,16384]{2,1,0:T(8,128)S(1)} fusion(f32[8,8,16384]{2,1,0:T(8,128)} %reshape.46, f32[8,8,16384]{2,1,0:T(8,128)} %add.50, f32[8]{0:T(128)S(1)} %get-tuple-element.84), kind=kLoop, calls=%fused_computation.2 | loop fusion | flops 2097152 | bytes 12582944 | tf_op jit(solution)/shard_map/add | solution.py:51
  56.7 2.4 %copy.17 = f32[8,8,16384]{2,0,1:T(8,128)S(1)} copy(f32[8,8,16384]{2,1,0:T(8,128)S(1)} %add_add_fusion) | data formatting | bytes 8388608 | tf_op jit(solution)/shard_map/add | solution.py:51
  59.1 52.6 %all_to_all.16 = f32[8,8,16384]{2,0,1:T(8,128)S(1)} all-to-all(f32[8,8,16384]{2,0,1:T(8,128)S(1)} %copy.17), channel_id=1, replica_groups=mesh['grp'=4,'dev'=8] {'dev'}, dimensions={1} | all-to-all | bytes 8388608 | tf_op jit(solution)/shard_map/all_to_all | solution.py:42
  111.7 2.0 %copy.26 = f32[64,16384]{1,0:T(8,128)} copy(f32[64,16384]{1,0:T(8,128)S(1)} %bitcast.16) | data formatting | bytes 8388608
  (7 shorter events, 0.1 us)
Async XLA Ops:
  32.7 5.0 %copy-start = (u32[32]{0:T(128)S(1)}, u32[32]{0:T(128)}, u32[]{:S(2)}) copy-start(u32[32]{0:T(128)} %constant.37) | copy-start | bytes 388
where the time goes:
time: 114 us
  blocking collectives  66 us (58%)
  local copies, waits for them, and re-layouts  28.2 us (25%)
  other arithmetic  10.6 us (9%)
  matrix products  8.18 us (7%)
    all_to_all x1, blocking collectives, relayout(): lax.all_to_all(values, 'dev', split_axis=1, concat_axis=0, tiled=True)  52.6 us
    unnamed x1, blocking collectives  13.5 us
    dot_general x1, matrix products, local_scan(): jnp.dot(blocks, upper_ones, precision=lax.Precision.HIGHEST, preferred_el...  8.18 us
    add x2, local copies, waits for them, and re-layouts, local_scan(): result = (within + starts[:, :, None]).reshape(chans, length)  7.34 us
    dot_general x1, local copies, waits for them, and re-layouts, local_scan(): jnp.dot(blocks, upper_ones, precision=lax.Precision.HIGHEST, preferred_el...  5.34 us
    reshape x1, local copies, waits for them, and re-layouts, local_scan(): blocks = values.reshape(chans * count, block_len)  4.95 us
    reshape x1, local copies, waits for them, and re-layouts, local_scan(): within = within.reshape(chans, count, block_len)  4.94 us
    add x1, other arithmetic, local(): result = relayout(partial_sums + chain_groups(column_sum)[:, None])  3.92 us

commit v1 on v0

--- a/solution.py
+++ b/solution.py
@@ -39,7 +39,10 @@
 
 
 def relayout(values):
-    return lax.all_to_all(values, "dev", split_axis=1, concat_axis=0, tiled=True)
+    return jnp.concatenate(
+        lax.all_to_all(jnp.stack(jnp.split(values, lax.axis_size("dev"), axis=1)), "dev", 0, 0),
+        axis=0,
+    )
 
 
 def chain_groups(column_sum):

time: 114 us -> 104 us (0.912)
  local copies, waits for them, and re-layouts: 28.2 us -> 20.9 us
  other arithmetic: 10.6 us -> 7.18 us
    add x2 -> x1, local copies, waits for them, and re-layouts: 7.34 us -> 0.33 us  [local_scan(): result = (within + starts[:, :, None]).reshape(chans, length)]
    add x1, other arithmetic: 3.92 us -> 0.49 us  [local(): result = relayout(partial_sums + chain_groups(column_sum)[:, None])]
    add x1 -> x0, local copies, waits for them, and re-layouts: 2.43 us -> none  [local(): result = relayout(partial_sums + chain_groups(column_sum)[:, None])]
    unnamed x6 -> x15, local copies, waits for them, and re-layouts: 2.86 us -> 4.97 us
where the time goes in v1:
time: 104 us; the launch traced here: 103 us
  blocking collectives  66 us (63%)
  local copies, waits for them, and re-layouts  20.9 us (20%)
  matrix products  8.18 us (8%)
  other arithmetic  7.18 us (7%)
    all_to_all x1, blocking collectives, relayout(): lax.all_to_all(jnp.stack(jnp.split(values, lax.axis_size('dev'), axis=1))...  52.6 us
    unnamed x1, blocking collectives  13.5 us
    dot_general x1, matrix products, local_scan(): jnp.dot(blocks, upper_ones, precision=lax.Precision.HIGHEST, preferred_el...  8.18 us
    dot_general x1, local copies, waits for them, and re-layouts, local_scan(): jnp.dot(blocks, upper_ones, precision=lax.Precision.HIGHEST, preferred_el...  5.34 us
    unnamed x15, local copies, waits for them, and re-layouts  4.97 us
    reshape x1, local copies, waits for them, and re-layouts, local_scan(): blocks = values.reshape(chans * count, block_len)  4.95 us
    reshape x1, local copies, waits for them, and re-layouts, local_scan(): within = within.reshape(chans, count, block_len)  4.86 us
    reduce_sum x1, other arithmetic, local_scan(): return (result, jnp.sum(sums, axis=1))  3.39 us

profile of v1, /device:TPU:0, one launch (start us, length us, event | category | flops | bytes accessed | tf_op | source)
XLA Modules:
  0.0 103.1 jit_solution(2181461945023686233)
XLA Ops:
  0.0 4.9 %reshape.38 = f32[2048,512]{1,0:T(8,128)} reshape(f32[8,131072]{1,0:T(8,128)} %param.3) | data formatting | bytes 8388608 | tf_op jit(solution)/shard_map/reshape | solution.py:26
  4.9 8.2 %convolution_bitcast_fusion = f32[2048,512]{0,1:T(8,128)} fusion(f32[2048,512]{1,0:T(8,128)} %reshape.38), kind=kOutput, calls=%fused_computation.3 | convolution fusion | flops 6442975232 | bytes 8388608 | tf_op jit(solution)/shard_map/dot_general | solution.py:27
  13.1 5.3 %copy.4 = f32[2048,512]{1,0:T(8,128)} copy(f32[2048,512]{0,1:T(8,128)} %convolution_bitcast_fusion) | data formatting | bytes 8388608 | tf_op jit(solution)/shard_map/dot_general | solution.py:27
  18.5 4.9 %reshape.39 = f32[8,131072]{1,0:T(8,128)} reshape(f32[2048,512]{1,0:T(8,128)} %copy.4) | data formatting | bytes 8388608 | tf_op jit(solution)/shard_map/reshape | solution.py:30
  23.3 0.0 copy-start.1
  23.3 3.4 %reduce_sum.19 = f32[8]{0:T(128)S(1)} reduce(f32[8,131072]{1,0:T(8,128)} %param.3, f32[]{:T(128)} %constant.32.clone.1), dimensions={1}, to_apply=%region_3.4 | reduce | flops 1048568 | bytes 4194340 | tf_op jit(solution)/shard_map/reduce_sum | solution.py:34
  26.7 2.5 %reduce_sum.18 = f32[8,256]{0,1:T(8,128)S(1)} reduce(f32[8,256,512]{2,0,1:T(8,128)} %bitcast.46, f32[]{:T(128)} %constant.32.clone.1), dimensions={2}, to_apply=%region_0.0 | reduce | flops 1046528 | bytes 4202500 | tf_op jit(solution)/shard_map/reduce_sum | solution.py:31
  29.3 0.1 copy.5
  29.3 0.6 reduce-window.6
  29.9 0.2 slice_reduce_fusion
  30.1 0.1 add_bitcast_fusion
  30.2 0.1 copy.6
  30.4 0.0 copy-done.1
  30.4 0.6 dynamic-slice
  31.6 0.2 dynamic-update-slice
  31.8 13.5 %all-reduce = f32[32]{0:T(128)S(1)} all-reduce(f32[32]{0:T(128)S(1)} %dynamic-update-slice), channel_id=2, replica_groups=mesh['grp'=4,'dev'=8] {'grp'}, use_global_device_ids=true, to_apply=%add | all-reduce | flops 32 | bytes 256
  45.3 0.1 reshape.44
  45.4 0.1 while.14
  45.5 0.0 copy-start
  45.5 0.3 add.47
  45.8 1.8 %copy-done = f32[8,131072]{1,0:T(8,128)S(1)} copy-done((f32[8,131072]{1,0:T(8,128)S(1)}, f32[8,131072]{1,0:T(8,128)}, u32[]{:S(2)}) %copy-start) | copy-done | bytes 4194328
  47.7 0.5 add_add_fusion
  48.5 52.6 %all_to_all.5 = f32[8,8,16384]{2,1,0:T(8,128)S(1)} all-to-all(f32[8,8,16384]{2,1,0:T(8,128)S(1)} %fusion.2), channel_id=1, replica_groups=mesh['grp'=4,'dev'=8] {'dev'}, dimensions={0} | all-to-all | bytes 8388608 | tf_op jit(solution)/shard_map/all_to_all | solution.py:43
  101.1 2.0 %copy.22 = f32[64,16384]{1,0:T(8,128)} copy(f32[64,16384]{1,0:T(8,128)S(1)} %bitcast.48) | data formatting | bytes 8388608
  (16 shorter events, 0.4 us)
Async XLA Ops:
  23.3 7.0 %copy-start.1 = (u32[32]{0:T(128)S(1)}, u32[32]{0:T(128)}, u32[]{:S(2)}) copy-start(u32[32]{0:T(128)} %constant.37) | copy-start | bytes 388
  45.5 2.2 %copy-start = (f32[8,131072]{1,0:T(8,128)S(1)}, f32[8,131072]{1,0:T(8,128)}, u32[]{:S(2)}) copy-start(f32[8,131072]{1,0:T(8,128)} %reshape.39) | copy-start | bytes 12582916
